TPU v7x, 128 devices: a whole 4x4x4 slice. The times are simulated.
128 devices in a mesh: genes: 64 (over z, y, x_hi, core), cols: 2 (over x_lo).
Axes of the slice: x: 4 (x_hi: 2, x_lo: 2; x = x_hi * 2 + x_lo), y: 4, z: 4, core: 2. Of those that a mesh axis runs over, the one named last changes fastest.
Arguments:
- expression: float32 [384, 40960], P(None, ('genes', 'cols')), may hold values from -200 to 200
- resample: int32 [384], replicated, may hold values from 0 to 383
- labels: int32 [40960, 300], P(('genes', 'cols')), may hold values from 0 to 1, as said below
- ref_kim: float32 [40960], P(('genes', 'cols')), may hold values from 0 to 1
Outputs:
- connectivity: float32 [40960, 300], P(('genes', 'cols'))
- preservation: float32 [2, 300], replicated
Inputs may be any that keep to these rules, and one draw needn't show every extreme that they name: `labels`: each row holds exactly one 1; every module has 32 or more genes.
All inputs are finite; a program needn't handle non-finite values.
Results may differ from a plain program's by a relative error of at most 0.0031.
Values may be sent and summed in bfloat16 or wider, within the bound.
A program may use at most 64 MiB of HBM per device.

v0:
```python
import math
import jax
import jax.numpy as jnp
from jax import lax
from jax.sharding import Mesh
from jax.sharding import PartitionSpec as P

G = 40960
GENES = ("genes_0", "genes_1", "genes_2", "genes_3")
GENES_COLS = ("genes_0", "genes_1", "genes_2", "genes_3", "cols")


def in_order(blocks, dim):
    lengths = list(blocks.shape[1:])
    lengths[dim] *= blocks.shape[0]
    return jnp.moveaxis(blocks, 0, dim).reshape(lengths)


def sent_to_all(x, axis):
    copies = jnp.broadcast_to(x, (lax.axis_size(axis), *x.shape))
    return lax.all_to_all(copies, axis, split_axis=0, concat_axis=0, tiled=True)


def gathered_copies(x, axis, dim):
    return in_order(sent_to_all(x, axis), dim)


def split_up(x, dim, count):
    before, after = (x.shape[:dim], x.shape[dim + 1 :])
    return jnp.moveaxis(x.reshape(*before, count, -1, *after), dim, 0)


def sum_at_owner(x, axis, dim):
    count = lax.axis_size(axis)
    blocks = lax.all_to_all(split_up(x, dim, count), axis, 0, 0, tiled=True)
    return jnp.sum(blocks.astype(jnp.float32), axis=0)


def one_axis_at_a_time(x, axes):
    for axis in axes:
        x = lax.psum(x, axis)
    return x


def standardize(expression, resample):
    boot = jnp.take(expression, resample, axis=0)
    centered = boot - jnp.mean(boot, axis=0, keepdims=True)
    total = jnp.sum(centered * centered, axis=0, keepdims=True)
    return (centered * lax.rsqrt(total + 1e-06)).astype(jnp.bfloat16)


def local_sums(connectivity, labels, ref_kim):
    member = labels.astype(jnp.float32)
    kim = jnp.sum(connectivity * member, axis=1)
    rowsum = jnp.sum(connectivity, axis=1)
    stacked = jnp.stack(
        [kim, kim * kim, ref_kim, ref_kim * ref_kim, kim * ref_kim, rowsum, jnp.ones_like(kim)],
        axis=1,
    )
    return jnp.dot(
        member.T, stacked, precision=lax.Precision.HIGHEST, preferred_element_type=jnp.float32
    )


def preserve(sums, total_genes):
    counts = sums[:, 6]
    mean_x = sums[:, 0] / (counts * counts)
    var_x = jnp.maximum(sums[:, 1] / (counts * counts * counts) - mean_x * mean_x, 0.0001)
    mean_y = sums[:, 2] / counts
    var_y = jnp.maximum(sums[:, 3] / counts - mean_y * mean_y, 0.01)
    cross = sums[:, 4] / (counts * counts) - mean_x * mean_y
    between = (sums[:, 5] - sums[:, 0]) / (counts * (total_genes - counts))
    density = (mean_x - between) * jnp.sqrt(counts / var_x)
    linked = cross * jnp.sqrt(counts / (var_x * var_y))
    return jnp.stack([density, linked], axis=0)


def tile_term(row_block, column_block, column_ids, module_count):
    scores = lax.dot_general(
        row_block, column_block, (((0,), (0,)), ((), ())), preferred_element_type=jnp.float32
    )
    squares = scores * scores
    adjacency = (squares * squares * squares).astype(jnp.bfloat16)
    member_block = (
        column_ids[:, None] == jnp.arange(module_count, dtype=jnp.int32)[None, :]
    ).astype(jnp.bfloat16)
    return jnp.dot(adjacency, member_block, preferred_element_type=jnp.float32)


def add_tiles(carried, row_block, piece, every_ids, shard_width, module_count):
    span_width = piece.shape[1]
    column_step = shard_width * math.gcd(span_width // shard_width, 8)
    steps_total = span_width // column_step

    def one_step(step_index, accumulated):
        columns = lax.dynamic_slice_in_dim(piece, step_index * column_step, column_step, 1)
        column_ids = lax.dynamic_slice_in_dim(every_ids, step_index * column_step, column_step, 0)
        return accumulated + tile_term(row_block, columns, column_ids, module_count)

    return lax.fori_loop(0, steps_total, one_step, carried)


def local(expression, resample, labels, ref_kim):
    scaled = standardize(expression, resample)
    module_count = labels.shape[1]
    shard_width = scaled.shape[1]
    module_ids = jnp.sum(labels * jnp.arange(module_count, dtype=jnp.int32)[None, :], axis=1)
    row_block = gathered_copies(scaled, "cols", 1)
    panel_ids = gathered_copies(module_ids, GENES, 0)
    initial = jnp.zeros((row_block.shape[1], module_count), jnp.float32)
    partial_value = add_tiles(
        initial,
        row_block,
        lax.all_gather(scaled, GENES, axis=1, tiled=True),
        panel_ids,
        shard_width,
        module_count,
    )
    connectivity = sum_at_owner(partial_value.astype(jnp.bfloat16), "cols", 0)
    sums = one_axis_at_a_time(local_sums(connectivity, labels, ref_kim), GENES_COLS)
    return (connectivity, preserve(sums, G))


def solution(mesh):
    torus = Mesh(
        mesh.devices.reshape(4, 4, 2, 2, mesh.shape["cols"]),
        ("genes_0", "genes_1", "genes_2", "genes_3", "cols"),
    )
    placed = (P(None, GENES_COLS), P(), P(GENES_COLS, None), P(GENES_COLS))
    return jax.shard_map(
        local, mesh=torus, in_specs=placed, out_specs=(P(GENES_COLS, None), P()), check_vma=False
    )
```

profile of v0, /device:TPU:2, one launch (start us, length us, event | category | flops | bytes accessed | tf_op | source)
XLA Modules:
  0.0 233.6 jit_solution(9748620751659558973)
XLA Ops:
  8.6 1.3 copy.21
  9.9 1.7 gather_fusion
  12.3 0.9 multiply_convert_fusion
  13.3 20.1 %all_to_all.16 = s32[64,1,320]{2,1,0:T(1,128)S(1)} all-to-all(s32[64,1,320]{2,1,0:T(1,128)S(1)} %broadcast_in_dim.35), channel_id=1, replica_groups=mesh['genes_0'=4,'genes_1'=4,'genes_2'=2,'genes_3'=2,'cols'=2] {'genes_0..., dimensions={0} | all-to-all | bytes 163840 | tf_op jit(solution)/shard_map/all_to_all | solution.py:21
  33.4 1.8 broadcast_in_dim.34
  35.1 4.9 %all-to-all-start = ((bf16[2,384,320]{1,2,0:T(8,128)(2,1)}), bf16[2,384,320]{1,2,0:T(8,128)(2,1)S(1)}, u32[]{:S(2)}, u32[]{:S(2)}) async-start(bf16[2,384,320]{1,2,0:T(8,128)(2,1)} %broadcast_in_dim.34), calls=%async_computation | async-start | bytes 983040 | tf_op jit(solution)/shard_map/all_to_all | solution.py:21
  40.4 6.0 %all-to-all-done = bf16[2,384,320]{1,2,0:T(8,128)(2,1)S(1)} async-done(((bf16[2,384,320]{1,2,0:T(8,128)(2,1)}), bf16[2,384,320]{1,2,0:T(8,128)(2,1)S(1)}, u32[]{:S(2)}, u32[]{:S(2)}) %all-to-all-start) | async-done | bytes 491552 | tf_op jit(solution)/shard_map/all_to_all | solution.py:21
  46.6 69.9 %all-gather.2.cloned.1.call-done = bf16[384,20480]{0,1:T(8,128)(2,1)} async-done(((bf16[384,320]{0,1:T(8,128)(2,1)}), bf16[384,20480]{0,1:T(8,128)(2,1)}) %all-gather.2.cloned.1.call-update) | async-done | bytes 15728656 | tf_op jit(solution)/shard_map/all_gather | solution.py:114
  116.5 43.6 %while.14 = (s32[]{:T(128)}, f32[640,300]{0,1:T(8,128)S(1)}, bf16[384,20480]{0,1:T(8,128)(2,1)}, bf16[384,640]{1,0:T(8,128)(2,1)S(1)}, s32[20480]{0:T(1024)S(1)}...) while((s32[]{:T(128)}, f32[640,300]{0,1:T(8,128)S(1)}, bf16[384,20480]{0,1:T(8,128)(2,1)}, ...), condition=%wide.region_4.5_spmd.clone, body=%wide.region_3.4_spmd.clone.sunk | while | flops 2249036800 | bytes 4024477 | solution.py:100
  116.6 5.3 %fusion.32 = f32[640,300]{0,1:T(8,128)S(1)} fusion(s32[2560]{0:T(1024)S(1)} %dynamic_slice.25, bf16[384,640]{1,0:T(8,128)(2,1)S(1)} %get-tuple-element.204, bf16[384,20480]{0,1:T(8,128)(2,1)} %get-tuple-element.203, s32[]{:T(128)S(6)} %select_n.27, f32[640,300]{0,1:T(8,128)S(1)} %get-tuple-element.193, pred[]{:T(512)S(6)} %compare.3), kind=kOutput, calls=%fused_computation.7.clone.1 | convolution fusion | flops 2249036800 | bytes 4003845 | tf_op jit(solution)/shard_map/while/body/eval_jaxpr/dot_general | solution.py:87
  122.1 5.3 %fusion.32 = f32[640,300]{0,1:T(8,128)S(1)} fusion(s32[2560]{0:T(1024)S(1)} %dynamic_slice.25, bf16[384,640]{1,0:T(8,128)(2,1)S(1)} %get-tuple-element.204, bf16[384,20480]{0,1:T(8,128)(2,1)} %get-tuple-element.203, s32[]{:T(128)S(6)} %select_n.27, f32[640,300]{0,1:T(8,128)S(1)} %get-tuple-element.193, pred[]{:T(512)S(6)} %compare.3), kind=kOutput, calls=%fused_computation.7.clone.1 | convolution fusion | flops 2249036800 | bytes 4003845 | tf_op jit(solution)/shard_map/while/body/eval_jaxpr/dot_general | solution.py:87
  127.5 5.3 %fusion.32 = f32[640,300]{0,1:T(8,128)S(1)} fusion(s32[2560]{0:T(1024)S(1)} %dynamic_slice.25, bf16[384,640]{1,0:T(8,128)(2,1)S(1)} %get-tuple-element.204, bf16[384,20480]{0,1:T(8,128)(2,1)} %get-tuple-element.203, s32[]{:T(128)S(6)} %select_n.27, f32[640,300]{0,1:T(8,128)S(1)} %get-tuple-element.193, pred[]{:T(512)S(6)} %compare.3), kind=kOutput, calls=%fused_computation.7.clone.1 | convolution fusion | flops 2249036800 | bytes 4003845 | tf_op jit(solution)/shard_map/while/body/eval_jaxpr/dot_general | solution.py:87
  133.0 5.3 %fusion.32 = f32[640,300]{0,1:T(8,128)S(1)} fusion(s32[2560]{0:T(1024)S(1)} %dynamic_slice.25, bf16[384,640]{1,0:T(8,128)(2,1)S(1)} %get-tuple-element.204, bf16[384,20480]{0,1:T(8,128)(2,1)} %get-tuple-element.203, s32[]{:T(128)S(6)} %select_n.27, f32[640,300]{0,1:T(8,128)S(1)} %get-tuple-element.193, pred[]{:T(512)S(6)} %compare.3), kind=kOutput, calls=%fused_computation.7.clone.1 | convolution fusion | flops 2249036800 | bytes 4003845 | tf_op jit(solution)/shard_map/while/body/eval_jaxpr/dot_general | solution.py:87
  138.4 5.3 %fusion.32 = f32[640,300]{0,1:T(8,128)S(1)} fusion(s32[2560]{0:T(1024)S(1)} %dynamic_slice.25, bf16[384,640]{1,0:T(8,128)(2,1)S(1)} %get-tuple-element.204, bf16[384,20480]{0,1:T(8,128)(2,1)} %get-tuple-element.203, s32[]{:T(128)S(6)} %select_n.27, f32[640,300]{0,1:T(8,128)S(1)} %get-tuple-element.193, pred[]{:T(512)S(6)} %compare.3), kind=kOutput, calls=%fused_computation.7.clone.1 | convolution fusion | flops 2249036800 | bytes 4003845 | tf_op jit(solution)/shard_map/while/body/eval_jaxpr/dot_general | solution.py:87
  143.9 5.3 %fusion.32 = f32[640,300]{0,1:T(8,128)S(1)} fusion(s32[2560]{0:T(1024)S(1)} %dynamic_slice.25, bf16[384,640]{1,0:T(8,128)(2,1)S(1)} %get-tuple-element.204, bf16[384,20480]{0,1:T(8,128)(2,1)} %get-tuple-element.203, s32[]{:T(128)S(6)} %select_n.27, f32[640,300]{0,1:T(8,128)S(1)} %get-tuple-element.193, pred[]{:T(512)S(6)} %compare.3), kind=kOutput, calls=%fused_computation.7.clone.1 | convolution fusion | flops 2249036800 | bytes 4003845 | tf_op jit(solution)/shard_map/while/body/eval_jaxpr/dot_general | solution.py:87
  149.3 5.3 %fusion.32 = f32[640,300]{0,1:T(8,128)S(1)} fusion(s32[2560]{0:T(1024)S(1)} %dynamic_slice.25, bf16[384,640]{1,0:T(8,128)(2,1)S(1)} %get-tuple-element.204, bf16[384,20480]{0,1:T(8,128)(2,1)} %get-tuple-element.203, s32[]{:T(128)S(6)} %select_n.27, f32[640,300]{0,1:T(8,128)S(1)} %get-tuple-element.193, pred[]{:T(512)S(6)} %compare.3), kind=kOutput, calls=%fused_computation.7.clone.1 | convolution fusion | flops 2249036800 | bytes 4003845 | tf_op jit(solution)/shard_map/while/body/eval_jaxpr/dot_general | solution.py:87
  154.8 5.3 %fusion.32 = f32[640,300]{0,1:T(8,128)S(1)} fusion(s32[2560]{0:T(1024)S(1)} %dynamic_slice.25, bf16[384,640]{1,0:T(8,128)(2,1)S(1)} %get-tuple-element.204, bf16[384,20480]{0,1:T(8,128)(2,1)} %get-tuple-element.203, s32[]{:T(128)S(6)} %select_n.27, f32[640,300]{0,1:T(8,128)S(1)} %get-tuple-element.193, pred[]{:T(512)S(6)} %compare.3), kind=kOutput, calls=%fused_computation.7.clone.1 | convolution fusion | flops 2249036800 | bytes 4003845 | tf_op jit(solution)/shard_map/while/body/eval_jaxpr/dot_general | solution.py:87
  161.5 5.0 %all-to-all-start.2 = ((bf16[2,320,300]{1,2,0:T(8,128)(2,1)}), bf16[2,320,300]{1,2,0:T(8,128)(2,1)S(1)}, u32[]{:S(2)}, u32[]{:S(2)}) async-start(bf16[2,320,300]{1,2,0:T(8,128)(2,1)} %copy.25), calls=%async_computation.2 | async-start | bytes 933888 | tf_op jit(solution)/shard_map/all_to_all | solution.py:35
  166.4 6.3 %all-to-all-done.2 = bf16[2,320,300]{1,2,0:T(8,128)(2,1)S(1)} async-done(((bf16[2,320,300]{1,2,0:T(8,128)(2,1)}), bf16[2,320,300]{1,2,0:T(8,128)(2,1)S(1)}, u32[]{:S(2)}, u32[]{:S(2)}) %all-to-all-start.2) | async-done | bytes 384032 | tf_op jit(solution)/shard_map/all_to_all | solution.py:35
  173.6 17.1 %psum.35 = f32[300,7]{0,1:T(8,128)S(1)} all-reduce(f32[300,7]{0,1:T(8,128)S(1)} %convolution_bitcast_fusion), channel_id=1, replica_groups=mesh['genes_0'=4,'genes_1'=4,'genes_2'=2,'genes_3'=2,'cols'=2] {'genes_0'}, use_global_device_ids=true, to_apply=%region_8.9 | all-reduce | flops 2100 | bytes 16800 | tf_op jit(solution)/shard_map/psum | solution.py:41
  190.7 14.9 %psum.36 = f32[300,7]{0,1:T(8,128)S(1)} all-reduce(f32[300,7]{0,1:T(8,128)S(1)} %psum.35), channel_id=1, replica_groups=mesh['genes_0'=4,'genes_1'=4,'genes_2'=2,'genes_3'=2,'cols'=2] {'genes_1'}, use_global_device_ids=true, to_apply=%region_9.10 | all-reduce | flops 2100 | bytes 16800 | tf_op jit(solution)/shard_map/psum | solution.py:41
  205.6 8.2 %psum.37 = f32[300,7]{0,1:T(8,128)S(1)} all-reduce(f32[300,7]{0,1:T(8,128)S(1)} %psum.36), channel_id=1, replica_groups=mesh['genes_0'=4,'genes_1'=4,'genes_2'=2,'genes_3'=2,'cols'=2] {'genes_2'}, use_global_device_ids=true, to_apply=%region_10.11 | all-reduce | flops 2100 | bytes 16800 | tf_op jit(solution)/shard_map/psum | solution.py:41
  213.8 3.3 %psum.38 = f32[300,7]{0,1:T(8,128)S(1)} all-reduce(f32[300,7]{0,1:T(8,128)S(1)} %psum.37), channel_id=1, replica_groups=mesh['genes_0'=4,'genes_1'=4,'genes_2'=2,'genes_3'=2,'cols'=2] {'genes_3'}, use_global_device_ids=true, to_apply=%region_11.12 | all-reduce | flops 2100 | bytes 16800 | tf_op jit(solution)/shard_map/psum | solution.py:41
  217.0 9.1 %psum.39 = f32[300,7]{0,1:T(8,128)S(1)} all-reduce(f32[300,7]{0,1:T(8,128)S(1)} %psum.38), channel_id=1, replica_groups=mesh['genes_0'=4,'genes_1'=4,'genes_2'=2,'genes_3'=2,'cols'=2] {'cols'}, use_global_device_ids=true, to_apply=%region_12.13 | all-reduce | flops 2100 | bytes 16800 | tf_op jit(solution)/shard_map/psum | solution.py:41
  (48 shorter events, 6.2 us)
Async XLA Ops:
  7.2 6.0 %copy-start = (s32[320,300]{0,1:T(8,128)S(1)}, s32[320,300]{0,1:T(8,128)}, u32[]{:S(2)}) copy-start(s32[320,300]{0,1:T(8,128)} %param.8) | copy-start | bytes 1152004
  7.2 109.3 %all-gather.2.cloned.1.call-start = ((), (), s32[]{:S(2)}) async-start(), calls=%async_computation.3 | async-start | bytes 15974400 | tf_op jit(solution)/shard_map/all_gather | solution.py:114
  35.1 11.2 %all-to-all-start = ((bf16[2,384,320]{1,2,0:T(8,128)(2,1)}), bf16[2,384,320]{1,2,0:T(8,128)(2,1)S(1)}, u32[]{:S(2)}, u32[]{:S(2)}) async-start(bf16[2,384,320]{1,2,0:T(8,128)(2,1)} %broadcast_in_dim.34), calls=%async_computation | async-start | bytes 983040 | tf_op jit(solution)/shard_map/all_to_all | solution.py:21
  116.5 49.9 %copy-start.2 = (f32[320]{0:T(512)S(1)}, f32[320]{0:T(512)}, u32[]{:S(2)}) copy-start(f32[320]{0:T(512)} %param.9) | copy-start | bytes 3844
  161.5 11.2 %all-to-all-start.2 = ((bf16[2,320,300]{1,2,0:T(8,128)(2,1)}), bf16[2,320,300]{1,2,0:T(8,128)(2,1)S(1)}, u32[]{:S(2)}, u32[]{:S(2)}) async-start(bf16[2,320,300]{1,2,0:T(8,128)(2,1)} %copy.25), calls=%async_computation.2 | async-start | bytes 933888 | tf_op jit(solution)/shard_map/all_to_all | solution.py:35
  172.9 53.8 %copy-start.1 = (f32[320,300]{0,1:T(8,128)}, f32[320,300]{0,1:T(8,128)S(1)}, u32[]{:S(2)}) copy-start(f32[320,300]{0,1:T(8,128)S(1)} %get-tuple-element.136) | copy-start | bytes 1152004
Sparse Core Ops, SparseCore 0:
  13.3 103.1 all-gather.1
where the time goes:
time: 234 us
  waiting for transfers between devices  82.2 us (35%)
  blocking collectives  72.6 us (31%)
  matrix products  43.2 us (18%)
  between operations  14.2 us (6%)
  starting transfers between devices  9.89 us (4%)
  local copies, waits for them, and re-layouts  7.35 us (3%)
  other arithmetic  4.01 us (2%)
    all_gather x1, waiting for transfers between devices, local(): lax.all_gather(scaled, GENES, axis=1, tiled=True)  69.9 us
    psum x5, blocking collectives, one_axis_at_a_time(): x = lax.psum(x, axis)  52.5 us
    dot_general x8, matrix products, tile_term(): return jnp.dot(adjacency, member_block, preferred_element_type=jnp.float32)  42.8 us
    all_to_all x1, blocking collectives, sent_to_all(): return lax.all_to_all(copies, axis, split_axis=0, concat_axis=0, tiled=True)  20.1 us
    all_to_all x1, waiting for transfers between devices, sum_at_owner(): blocks = lax.all_to_all(split_up(x, dim, count), axis, 0, 0, tiled=True)  6.29 us
    all_to_all x1, waiting for transfers between devices, sent_to_all(): return lax.all_to_all(copies, axis, split_axis=0, concat_axis=0, tiled=True)  5.99 us
    all_to_all x1, starting transfers between devices, sum_at_owner(): blocks = lax.all_to_all(split_up(x, dim, count), axis, 0, 0, tiled=True)  4.95 us
    all_to_all x1, starting transfers between devices, sent_to_all(): return lax.all_to_all(copies, axis, split_axis=0, concat_axis=0, tiled=True)  4.9 us
  transfers between devices with their start and end apart: 3, of which 3 were waited for; matrix products, arithmetic and copies ran while one was open for 1% of the time, Pallas kernels for 0%

commit v1 on v0

--- a/solution.py
+++ b/solution.py
@@ -4,6 +4,7 @@
 from jax import lax
 from jax.sharding import Mesh
 from jax.sharding import PartitionSpec as P
+from jax.lax import all_to_all, axis_size
 
 G = 40960
 GENES = ("genes_0", "genes_1", "genes_2", "genes_3")
@@ -111,7 +112,7 @@
     partial_value = add_tiles(
         initial,
         row_block,
-        lax.all_gather(scaled, GENES, axis=1, tiled=True),
+        jnp.concatenate(all_to_all(jnp.stack(axis_size(GENES) * [scaled], 0), GENES, 0, 0), 1),
         panel_ids,
         shard_width,
         module_count,

time: 234 us -> 388 us (1.66)
  waiting for transfers between devices: 82.2 us -> 211 us
  blocking collectives: 72.6 us -> 91.4 us
  starting transfers between devices: 9.89 us -> 24.2 us
  between operations: 14.2 us -> 0.8 us
  local copies, waits for them, and re-layouts: 7.35 us -> 11.9 us
    all_to_all x0 -> x1, waiting for transfers between devices: none -> 201 us  [local(): all_to_all(jnp.stack(axis_size(GENES) * [scaled], 0), GENES, 0, 0)]
    all_gather x1 -> x0, waiting for transfers between devices: 69.9 us -> none  [local(): lax.all_gather(scaled, GENES, axis=1, tiled=True)]
    psum x5, blocking collectives: 52.5 us -> 81.3 us  [one_axis_at_a_time(): x = lax.psum(x, axis)]
    all_to_all x1, blocking collectives: 20.1 us -> 10.2 us  [sent_to_all(): return lax.all_to_all(copies, axis, split_axis=0, concat_axis=0, tiled=True)]
    all_to_all x0 -> x1, starting transfers between devices: none -> 5.81 us  [local(): all_to_all(jnp.stack(axis_size(GENES) * [scaled], 0), GENES, 0, 0)]
    another operation x0 -> x1, local copies, waits for them, and re-layouts: none -> 5.63 us  [local(): jnp.stack(axis_size(GENES) * [scaled], 0)]
    all_to_all x1, starting transfers between devices: 4.9 us -> 10.5 us  [sent_to_all(): return lax.all_to_all(copies, axis, split_axis=0, concat_axis=0, tiled=True)]
where the time goes in v1:
time: 388 us; the launch traced here: 387 us
  waiting for transfers between devices  211 us (54%)
  blocking collectives  91.4 us (24%)
  matrix products  43.2 us (11%)
  starting transfers between devices  24.2 us (6%)
  local copies, waits for them, and re-layouts  11.9 us (3%)
  other arithmetic  4.29 us (1%)
    all_to_all x1, waiting for transfers between devices, local(): all_to_all(jnp.stack(axis_size(GENES) * [scaled], 0), GENES, 0, 0)  201 us
    psum x5, blocking collectives, one_axis_at_a_time(): x = lax.psum(x, axis)  81.3 us
    dot_general x8, matrix products, tile_term(): return jnp.dot(adjacency, member_block, preferred_element_type=jnp.float32)  42.8 us
    all_to_all x1, starting transfers between devices, sent_to_all(): return lax.all_to_all(copies, axis, split_axis=0, concat_axis=0, tiled=True)  10.5 us
    all_to_all x1, blocking collectives, sent_to_all(): return lax.all_to_all(copies, axis, split_axis=0, concat_axis=0, tiled=True)  10.2 us
    all_to_all x1, starting transfers between devices, sum_at_owner(): blocks = lax.all_to_all(split_up(x, dim, count), axis, 0, 0, tiled=True)  7.85 us
  transfers between devices with their start and end apart: 3, of which 3 were waited for; matrix products, arithmetic and copies ran while one was open for 1% of the time, Pallas kernels for 0%

profile of v1, /device:TPU:2, one launch (start us, length us, event | category | flops | bytes accessed | tf_op | source)
XLA Modules:
  0.0 386.9 jit_solution(4037379314416334715)
XLA Ops:
  2.4 10.5 %all-to-all-start.2 = ((s32[64,1,320]{2,1,0:T(1,128)}), s32[64,1,320]{2,1,0:T(1,128)S(1)}, u32[]{:S(2)}, u32[]{:S(2)}) async-start(s32[64,1,320]{2,1,0:T(1,128)} %broadcast_in_dim.35), calls=%async_computation.2 | async-start | bytes 196608 | tf_op jit(solution)/shard_map/all_to_all | solution.py:22
  14.3 1.3 copy.23
  15.6 1.7 gather_fusion
  18.1 4.6 %all-to-all-done.2 = s32[64,1,320]{2,1,0:T(1,128)S(1)} async-done(((s32[64,1,320]{2,1,0:T(1,128)}), s32[64,1,320]{2,1,0:T(1,128)S(1)}, u32[]{:S(2)}, u32[]{:S(2)}) %all-to-all-start.2) | async-done | bytes 81952 | tf_op jit(solution)/shard_map/all_to_all | solution.py:22
  22.8 10.2 %all_to_all.21 = bf16[2,384,320]{1,2,0:T(8,128)(2,1)S(1)} all-to-all(bf16[2,384,320]{1,2,0:T(8,128)(2,1)S(1)} %broadcast_in_dim.34), channel_id=1, replica_groups=mesh['genes_0'=4,'genes_1'=4,'genes_2'=2,'genes_3'=2,'cols'=2] {'cols'}, dimensions={0} | all-to-all | bytes 983040 | tf_op jit(solution)/shard_map/all_to_all | solution.py:22
  32.9 5.6 %stack.16 = bf16[64,384,320]{1,2,0:T(8,128)(2,1)} broadcast(bf16[384,320]{0,1:T(8,128)(2,1)S(1)} %multiply_convert_fusion), dimensions={1,2} | broadcast | bytes 15974400 | tf_op jit(solution)/shard_map/stack | solution.py:115
  38.5 5.8 %all-to-all-start = ((bf16[64,384,320]{1,2,0:T(8,128)(2,1)}), bf16[64,384,320]{1,2,0:T(8,128)(2,1)}, u32[]{:S(2)}, u32[]{:S(2)}) async-start(bf16[64,384,320]{1,2,0:T(8,128)(2,1)} %stack.16), calls=%async_computation | async-start | bytes 31457280 | tf_op jit(solution)/shard_map/all_to_all | solution.py:115
  45.0 200.6 %all-to-all-done = bf16[64,384,320]{1,2,0:T(8,128)(2,1)} async-done(((bf16[64,384,320]{1,2,0:T(8,128)(2,1)}), bf16[64,384,320]{1,2,0:T(8,128)(2,1)}, u32[]{:S(2)}, u32[]{:S(2)}) %all-to-all-start) | async-done | bytes 15728672 | tf_op jit(solution)/shard_map/all_to_all | solution.py:115
  245.5 43.7 %while.14 = (s32[]{:T(128)}, f32[640,300]{0,1:T(8,128)S(1)}, bf16[384,20480]{0,1:T(8,128)(2,1)}, bf16[384,640]{1,0:T(8,128)(2,1)S(1)}, s32[20480]{0:T(1024)S(1)}...) while((s32[]{:T(128)}, f32[640,300]{0,1:T(8,128)S(1)}, bf16[384,20480]{0,1:T(8,128)(2,1)}, ...), condition=%wide.region_4.5_spmd.clone, body=%wide.region_3.4_spmd.clone.sunk | while | flops 2249036800 | bytes 4024477 | solution.py:101
  245.6 5.4 %fusion.32 = f32[640,300]{0,1:T(8,128)S(1)} fusion(s32[2560]{0:T(1024)S(1)} %dynamic_slice.25, bf16[384,640]{1,0:T(8,128)(2,1)S(1)} %get-tuple-element.204, bf16[384,20480]{0,1:T(8,128)(2,1)} %get-tuple-element.203, s32[]{:T(128)S(6)} %select_n.29, f32[640,300]{0,1:T(8,128)S(1)} %get-tuple-element.193, pred[]{:T(512)S(6)} %compare.3), kind=kOutput, calls=%fused_computation.7.clone.1 | convolution fusion | flops 2249036800 | bytes 4003845 | tf_op jit(solution)/shard_map/while/body/eval_jaxpr/dot_general | solution.py:88
  251.1 5.3 %fusion.32 = f32[640,300]{0,1:T(8,128)S(1)} fusion(s32[2560]{0:T(1024)S(1)} %dynamic_slice.25, bf16[384,640]{1,0:T(8,128)(2,1)S(1)} %get-tuple-element.204, bf16[384,20480]{0,1:T(8,128)(2,1)} %get-tuple-element.203, s32[]{:T(128)S(6)} %select_n.29, f32[640,300]{0,1:T(8,128)S(1)} %get-tuple-element.193, pred[]{:T(512)S(6)} %compare.3), kind=kOutput, calls=%fused_computation.7.clone.1 | convolution fusion | flops 2249036800 | bytes 4003845 | tf_op jit(solution)/shard_map/while/body/eval_jaxpr/dot_general | solution.py:88
  256.6 5.3 %fusion.32 = f32[640,300]{0,1:T(8,128)S(1)} fusion(s32[2560]{0:T(1024)S(1)} %dynamic_slice.25, bf16[384,640]{1,0:T(8,128)(2,1)S(1)} %get-tuple-element.204, bf16[384,20480]{0,1:T(8,128)(2,1)} %get-tuple-element.203, s32[]{:T(128)S(6)} %select_n.29, f32[640,300]{0,1:T(8,128)S(1)} %get-tuple-element.193, pred[]{:T(512)S(6)} %compare.3), kind=kOutput, calls=%fused_computation.7.clone.1 | convolution fusion | flops 2249036800 | bytes 4003845 | tf_op jit(solution)/shard_map/while/body/eval_jaxpr/dot_general | solution.py:88
  262.0 5.3 %fusion.32 = f32[640,300]{0,1:T(8,128)S(1)} fusion(s32[2560]{0:T(1024)S(1)} %dynamic_slice.25, bf16[384,640]{1,0:T(8,128)(2,1)S(1)} %get-tuple-element.204, bf16[384,20480]{0,1:T(8,128)(2,1)} %get-tuple-element.203, s32[]{:T(128)S(6)} %select_n.29, f32[640,300]{0,1:T(8,128)S(1)} %get-tuple-element.193, pred[]{:T(512)S(6)} %compare.3), kind=kOutput, calls=%fused_computation.7.clone.1 | convolution fusion | flops 2249036800 | bytes 4003845 | tf_op jit(solution)/shard_map/while/body/eval_jaxpr/dot_general | solution.py:88
  267.5 5.3 %fusion.32 = f32[640,300]{0,1:T(8,128)S(1)} fusion(s32[2560]{0:T(1024)S(1)} %dynamic_slice.25, bf16[384,640]{1,0:T(8,128)(2,1)S(1)} %get-tuple-element.204, bf16[384,20480]{0,1:T(8,128)(2,1)} %get-tuple-element.203, s32[]{:T(128)S(6)} %select_n.29, f32[640,300]{0,1:T(8,128)S(1)} %get-tuple-element.193, pred[]{:T(512)S(6)} %compare.3), kind=kOutput, calls=%fused_computation.7.clone.1 | convolution fusion | flops 2249036800 | bytes 4003845 | tf_op jit(solution)/shard_map/while/body/eval_jaxpr/dot_general | solution.py:88
  272.9 5.3 %fusion.32 = f32[640,300]{0,1:T(8,128)S(1)} fusion(s32[2560]{0:T(1024)S(1)} %dynamic_slice.25, bf16[384,640]{1,0:T(8,128)(2,1)S(1)} %get-tuple-element.204, bf16[384,20480]{0,1:T(8,128)(2,1)} %get-tuple-element.203, s32[]{:T(128)S(6)} %select_n.29, f32[640,300]{0,1:T(8,128)S(1)} %get-tuple-element.193, pred[]{:T(512)S(6)} %compare.3), kind=kOutput, calls=%fused_computation.7.clone.1 | convolution fusion | flops 2249036800 | bytes 4003845 | tf_op jit(solution)/shard_map/while/body/eval_jaxpr/dot_general | solution.py:88
  278.4 5.3 %fusion.32 = f32[640,300]{0,1:T(8,128)S(1)} fusion(s32[2560]{0:T(1024)S(1)} %dynamic_slice.25, bf16[384,640]{1,0:T(8,128)(2,1)S(1)} %get-tuple-element.204, bf16[384,20480]{0,1:T(8,128)(2,1)} %get-tuple-element.203, s32[]{:T(128)S(6)} %select_n.29, f32[640,300]{0,1:T(8,128)S(1)} %get-tuple-element.193, pred[]{:T(512)S(6)} %compare.3), kind=kOutput, calls=%fused_computation.7.clone.1 | convolution fusion | flops 2249036800 | bytes 4003845 | tf_op jit(solution)/shard_map/while/body/eval_jaxpr/dot_general | solution.py:88
  283.8 5.3 %fusion.32 = f32[640,300]{0,1:T(8,128)S(1)} fusion(s32[2560]{0:T(1024)S(1)} %dynamic_slice.25, bf16[384,640]{1,0:T(8,128)(2,1)S(1)} %get-tuple-element.204, bf16[384,20480]{0,1:T(8,128)(2,1)} %get-tuple-element.203, s32[]{:T(128)S(6)} %select_n.29, f32[640,300]{0,1:T(8,128)S(1)} %get-tuple-element.193, pred[]{:T(512)S(6)} %compare.3), kind=kOutput, calls=%fused_computation.7.clone.1 | convolution fusion | flops 2249036800 | bytes 4003845 | tf_op jit(solution)/shard_map/while/body/eval_jaxpr/dot_general | solution.py:88
  290.5 7.8 %all-to-all-start.3 = ((bf16[2,320,300]{1,2,0:T(8,128)(2,1)}), bf16[2,320,300]{1,2,0:T(8,128)(2,1)S(1)}, u32[]{:S(2)}, u32[]{:S(2)}) async-start(bf16[2,320,300]{1,2,0:T(8,128)(2,1)} %copy.27), calls=%async_computation.3 | async-start | bytes 933888 | tf_op jit(solution)/shard_map/all_to_all | solution.py:36
  298.4 5.7 %all-to-all-done.3 = bf16[2,320,300]{1,2,0:T(8,128)(2,1)S(1)} async-done(((bf16[2,320,300]{1,2,0:T(8,128)(2,1)}), bf16[2,320,300]{1,2,0:T(8,128)(2,1)S(1)}, u32[]{:S(2)}, u32[]{:S(2)}) %all-to-all-start.3) | async-done | bytes 384032 | tf_op jit(solution)/shard_map/all_to_all | solution.py:36
  304.9 16.0 %psum.35 = f32[300,7]{0,1:T(8,128)S(1)} all-reduce(f32[300,7]{0,1:T(8,128)S(1)} %convolution_bitcast_fusion), channel_id=1, replica_groups=mesh['genes_0'=4,'genes_1'=4,'genes_2'=2,'genes_3'=2,'cols'=2] {'genes_0'}, use_global_device_ids=true, to_apply=%region_8.9 | all-reduce | flops 2100 | bytes 16800 | tf_op jit(solution)/shard_map/psum | solution.py:42
  320.9 21.2 %psum.36 = f32[300,7]{0,1:T(8,128)S(1)} all-reduce(f32[300,7]{0,1:T(8,128)S(1)} %psum.35), channel_id=1, replica_groups=mesh['genes_0'=4,'genes_1'=4,'genes_2'=2,'genes_3'=2,'cols'=2] {'genes_1'}, use_global_device_ids=true, to_apply=%region_9.10 | all-reduce | flops 2100 | bytes 16800 | tf_op jit(solution)/shard_map/psum | solution.py:42
  342.1 31.7 %psum.37 = f32[300,7]{0,1:T(8,128)S(1)} all-reduce(f32[300,7]{0,1:T(8,128)S(1)} %psum.36), channel_id=1, replica_groups=mesh['genes_0'=4,'genes_1'=4,'genes_2'=2,'genes_3'=2,'cols'=2] {'genes_2'}, use_global_device_ids=true, to_apply=%region_10.11 | all-reduce | flops 2100 | bytes 16800 | tf_op jit(solution)/shard_map/psum | solution.py:42
  373.7 3.3 psum.38
  377.0 9.2 %psum.39 = f32[300,7]{0,1:T(8,128)S(1)} all-reduce(f32[300,7]{0,1:T(8,128)S(1)} %psum.38), channel_id=1, replica_groups=mesh['genes_0'=4,'genes_1'=4,'genes_2'=2,'genes_3'=2,'cols'=2] {'cols'}, use_global_device_ids=true, to_apply=%region_12.13 | all-reduce | flops 2100 | bytes 16800 | tf_op jit(solution)/shard_map/psum | solution.py:42
  (48 shorter events, 8.0 us)
Async XLA Ops:
  2.4 20.3 %all-to-all-start.2 = ((s32[64,1,320]{2,1,0:T(1,128)}), s32[64,1,320]{2,1,0:T(1,128)S(1)}, u32[]{:S(2)}, u32[]{:S(2)}) async-start(s32[64,1,320]{2,1,0:T(1,128)} %broadcast_in_dim.35), calls=%async_computation.2 | async-start | bytes 196608 | tf_op jit(solution)/shard_map/all_to_all | solution.py:22
  38.5 207.0 %all-to-all-start = ((bf16[64,384,320]{1,2,0:T(8,128)(2,1)}), bf16[64,384,320]{1,2,0:T(8,128)(2,1)}, u32[]{:S(2)}, u32[]{:S(2)}) async-start(bf16[64,384,320]{1,2,0:T(8,128)(2,1)} %stack.16), calls=%async_computation | async-start | bytes 31457280 | tf_op jit(solution)/shard_map/all_to_all | solution.py:115
  245.5 52.8 %copy-start.2 = (f32[320]{0:T(512)S(1)}, f32[320]{0:T(512)}, u32[]{:S(2)}) copy-start(f32[320]{0:T(512)} %param.9) | copy-start | bytes 3844
  245.5 58.7 %copy-start = (s32[320,300]{0,1:T(8,128)S(1)}, s32[320,300]{0,1:T(8,128)}, u32[]{:S(2)}) copy-start(s32[320,300]{0,1:T(8,128)} %param.8) | copy-start | bytes 1152004
  290.5 13.5 %all-to-all-start.3 = ((bf16[2,320,300]{1,2,0:T(8,128)(2,1)}), bf16[2,320,300]{1,2,0:T(8,128)(2,1)S(1)}, u32[]{:S(2)}, u32[]{:S(2)}) async-start(bf16[2,320,300]{1,2,0:T(8,128)(2,1)} %copy.27), calls=%async_computation.3 | async-start | bytes 933888 | tf_op jit(solution)/shard_map/all_to_all | solution.py:36
  304.3 82.6 %copy-start.1 = (f32[320,300]{0,1:T(8,128)}, f32[320,300]{0,1:T(8,128)S(1)}, u32[]{:S(2)}) copy-start(f32[320,300]{0,1:T(8,128)S(1)} %get-tuple-element.136) | copy-start | bytes 1152004
